TPU v7x, 32 devices: a whole 2x2x4 slice. The times are simulated.
32 devices in a mesh: tmpl: 8 (over y, x, core), grid: 4 (over z).
Axes of the slice: x: 2, y: 2, z: 4, core: 2. Of those that a mesh axis runs over, the one named last changes fastest.
Arguments:
- spectrum: float32 [256, 64, 64, 128], P('tmpl', 'grid'), may hold values from -12 to 12
Outputs:
- best_scores: float32 [4, 64, 64, 64], P(None, 'grid', 'tmpl')
- coherence: float32 [64, 64, 64], P('grid', 'tmpl')
All inputs are finite; a program needn't handle non-finite values.
Results may differ from a plain program's by a relative error of at most 0.0001.
Values sent between devices are 32-bit elements; how exact they have to be, the bound alone decides.
A program may use at most 128 MiB of HBM per device.

v0:
```python
import math

import jax
import jax.numpy as jnp
from jax import lax
from jax.sharding import PartitionSpec as P

TOP = 4


FLOOR = -1e30
SPREAD_FLOOR = 0.25


def merged(value, axis, join):
    pieces = jax.tree.map(lambda part: lax.all_gather(part, axis), value)
    head = jax.tree.map(lambda part: part[0], pieces)
    tail = jax.tree.map(lambda part: part[1:], pieces)
    running, _ = lax.scan(lambda running, share: (join(running, share), None), head, tail)
    return running


def phase_table(length):
    order = jnp.arange(length, dtype=jnp.int32)
    turns = order[:, None] * order[None, :] % length
    angle = turns.astype(jnp.float32) * (2.0 * math.pi / length)
    return jnp.concatenate([jnp.cos(angle), -jnp.sin(angle)], axis=0)


def merge_top(former, latter):
    result = []
    for rank_out in range(len(former)):
        winner = jnp.maximum(former[rank_out], latter[rank_out])
        for rank_in in range(rank_out):
            winner = jnp.maximum(
                winner, jnp.minimum(former[rank_in], latter[rank_out - rank_in - 1])
            )
        result.append(winner)
    return tuple(result)


def fold_levels(leaders, running):
    while leaders[0].shape[0] > 1:
        number = leaders[0].shape[0]
        paired = tuple((value.reshape((number // 2, 2) + value.shape[1:]) for value in leaders))
        leaders = merge_top(
            tuple((value[:, 0] for value in paired)), tuple((value[:, 1] for value in paired))
        )
        folded = running.reshape((number // 2, 2) + running.shape[1:])
        running = folded[:, 0] + folded[:, 1]
    return (tuple((value[0] for value in leaders)), running[0])


def combine_groups(former, latter):
    leaders = merge_top(former[:-1], latter[:-1])
    return leaders + (former[-1] + latter[-1],)


def body(spectrum):
    local_tmpl, slab_rows, beta_rows, doubled = spectrum.shape
    points = doubled // 2
    paired_table = jnp.kron(jnp.eye(2, dtype=jnp.float32), phase_table(points))
    flat_rows = slab_rows * beta_rows // 2
    score = jnp.dot(
        spectrum.reshape(local_tmpl * flat_rows, 2 * doubled),
        paired_table,
        precision=lax.Precision.HIGHEST,
        preferred_element_type=jnp.float32,
    )
    score = score.reshape(local_tmpl, flat_rows, doubled)
    cell_count = float(points * points * points)
    sum_plain = jnp.sum(score, axis=(1, 2))
    sum_square = jnp.sum(score * score, axis=(1, 2))
    sum_plain, sum_square = lax.psum((sum_plain, sum_square), "grid")
    average = sum_plain / cell_count
    spread = sum_square / cell_count - average * average
    centred = score - average[:, None, None]
    normed = centred / jnp.sqrt(spread + SPREAD_FLOOR)[:, None, None]
    filler = jnp.full_like(normed, FLOOR)
    start = (normed,) + tuple((filler for rank_in in range(TOP - 1)))
    leaders, running = fold_levels(start, normed)
    line = beta_rows * points
    leaders = tuple((value.reshape(slab_rows, line) for value in leaders))
    running = running.reshape(slab_rows, line)
    groups = lax.axis_size("tmpl")
    piece = beta_rows // groups
    combined = merged(leaders + (running,), "tmpl", combine_groups)
    offset = lax.axis_index("tmpl") * (piece * points)
    owned = tuple(
        (lax.dynamic_slice_in_dim(value, offset, piece * points, 1) for value in combined)
    )
    best_parts, total_part = (owned[:-1], owned[-1])
    best_scores = jnp.stack(best_parts, axis=0).reshape(TOP, slab_rows, piece, points)
    coherence = (total_part / math.sqrt(groups * local_tmpl)).reshape(slab_rows, piece, points)
    return (best_scores, coherence)


def solution(mesh):
    return jax.shard_map(
        body,
        mesh=mesh,
        in_specs=(P("tmpl", "grid", None, None),),
        out_specs=(P(None, "grid", "tmpl", None), P("grid", "tmpl", None)),
        check_vma=False,
    )
```

profile of v0, /device:TPU:1, one launch (start us, length us, event | category | flops | bytes accessed | tf_op | source)
XLA Modules:
  0.0 270.3 jit_solution(18397949942095516304)
XLA Ops:
  7.4 19.1 %reshape.680 = f32[16384,256]{1,0:T(8,128)} reshape(f32[32,16,64,128]{3,2,1,0:T(8,128)} %param.3) | data formatting | bytes 33554432 | tf_op jit(solution)/shard_map/reshape | solution.py:65
  26.6 22.6 %multiply_reduce_fusion = (f32[16384]{0:T(1024)S(1)}, f32[128,16384]{1,0:T(8,128)}) fusion(f32[16384,256]{1,0:T(8,128)} %reshape.680, f32[16,8,2,128]{3,2,1,0:T(2,128)S(1)} %bitcast.207), kind=kOutput, calls=%fused_computation.17 | convolution fusion | flops 6446628864 | bytes 25362432 | tf_op jit(solution)/shard_map/dot_general | solution.py:64
  49.2 3.9 %reduce_sum.23 = f32[16384]{0:T(1024)S(1)} reduce(f32[128,16384]{1,0:T(8,128)} %get-tuple-element.117, f32[]{:T(128)} %constant.43.clone.1), dimensions={0}, to_apply=%region_0.1 | reduce | flops 2080768 | bytes 8454148 | tf_op jit(solution)/shard_map/reduce_sum | solution.py:72
  53.3 10.9 %all-reduce = (f32[32]{0:T(128)S(1)}, f32[32]{0:T(128)S(1)}) all-reduce(f32[32]{0:T(128)S(1)} %reduce_sum.37, f32[32]{0:T(128)S(1)} %reduce_sum.25), channel_id=1, replica_groups=mesh['tmpl'=8,'grid'=4] {'grid'}, use_global_device_ids=true, to_apply=%region_5.6 | all-reduce | flops 64 | bytes 512 | tf_op jit(solution)/shard_map/psum | solution.py:74
  64.6 11.8 %reshape.681 = f32[16,2,512,128]{2,1,0,3:T(2,128)} reshape(f32[16384,128]{0,1:T(8,128)} %bitcast.188) | data formatting | bytes 16777216 | tf_op jit(solution)/shard_map/reshape | solution.py:70
  76.4 13.2 %copy.58 = f32[16,2,512,128]{3,2,0,1:T(8,128)} copy(f32[16,2,512,128]{2,1,0,3:T(2,128)} %reshape.681) | data formatting | bytes 16777216 | tf_op jit(solution)/shard_map/reshape | solution.py:70
  89.5 4.5 %subtract_divide_fusion = f32[16,2,512,128]{3,2,0,1:T(8,128)S(1)} fusion(f32[16,2,512,128]{3,2,0,1:T(8,128)} %copy.58, f32[16,2]{0,1:T(2,128)S(1)} %copy.59, f32[16,2]{0,1:T(2,128)S(1)} %copy.57), kind=kLoop, calls=%fused_computation.18 | loop fusion | flops 4194304 | bytes 16777472 | tf_op jit(solution)/shard_map/div | solution.py:78
  94.0 2.6 slice_add_fusion
  102.6 2.4 slice_add_fusion.1
  106.1 22.6 %all-gather.8.cloned.1.call-done = f32[8,16,4096]{2,1,0:T(8,128)} async-done(((f32[1,16,4096]{2,1,0:T(8,128)}), f32[8,16,4096]{2,1,0:T(8,128)}) %all-gather.8.cloned.1.call-update) | async-done | bytes 2097168 | tf_op jit(solution)/shard_map/all_gather | solution.py:16
  128.6 29.7 %all-gather.10.cloned.1.call-done = f32[8,16,4096]{2,1,0:T(8,128)} async-done(((f32[1,16,4096]{2,1,0:T(8,128)}), f32[8,16,4096]{2,1,0:T(8,128)}) %all-gather.10.cloned.1.call-update) | async-done | bytes 2097168 | tf_op jit(solution)/shard_map/all_gather | solution.py:16
  158.3 2.9 %slice.251 = f32[7,16,4096]{2,1,0:T(8,128)} slice(f32[8,16,4096]{2,1,0:T(8,128)} %all-gather.10.cloned.1.call-done), slice={[1:8], [0:16], [0:4096]} | slice | bytes 3670016 | tf_op jit(solution)/shard_map/slice | solution.py:18
  161.2 26.8 %all-gather.12.cloned.1.call-done = f32[8,16,4096]{2,1,0:T(8,128)} async-done(((f32[1,16,4096]{2,1,0:T(8,128)}), f32[8,16,4096]{2,1,0:T(8,128)}) %all-gather.12.cloned.1.call-update) | async-done | bytes 2097168 | tf_op jit(solution)/shard_map/all_gather | solution.py:16
  188.0 2.9 %slice.252 = f32[7,16,4096]{2,1,0:T(8,128)} slice(f32[8,16,4096]{2,1,0:T(8,128)} %all-gather.12.cloned.1.call-done), slice={[1:8], [0:16], [0:4096]} | slice | bytes 3670016 | tf_op jit(solution)/shard_map/slice | solution.py:18
  190.9 27.2 %all-gather.6.cloned.1.call-done = f32[8,16,4096]{2,1,0:T(8,128)} async-done(((f32[1,16,4096]{2,1,0:T(8,128)}), f32[8,16,4096]{2,1,0:T(8,128)}) %all-gather.6.cloned.1.call-update) | async-done | bytes 2097168 | tf_op jit(solution)/shard_map/all_gather | solution.py:16
  218.2 2.9 %slice.249 = f32[7,16,4096]{2,1,0:T(8,128)} slice(f32[8,16,4096]{2,1,0:T(8,128)} %all-gather.6.cloned.1.call-done), slice={[1:8], [0:16], [0:4096]} | slice | bytes 3670016 | tf_op jit(solution)/shard_map/slice | solution.py:18
  224.0 23.7 %all-gather.14.cloned.1.call-done = f32[8,16,4096]{2,1,0:T(8,128)} async-done(((f32[1,16,4096]{2,1,0:T(8,128)}), f32[8,16,4096]{2,1,0:T(8,128)}) %all-gather.14.cloned.1.call-update) | async-done | bytes 2097168 | tf_op jit(solution)/shard_map/all_gather | solution.py:16
  247.7 2.9 %slice.253 = f32[7,16,4096]{2,1,0:T(8,128)} slice(f32[8,16,4096]{2,1,0:T(8,128)} %all-gather.14.cloned.1.call-done), slice={[1:8], [0:16], [0:4096]} | slice | bytes 3670016 | tf_op jit(solution)/shard_map/slice | solution.py:18
  251.6 10.4 %while.18 = (s32[]{:T(128)}, f32[16,4096]{1,0:T(8,128)S(1)}, f32[16,4096]{1,0:T(8,128)S(1)}, f32[16,4096]{1,0:T(8,128)S(1)}, f32[16,4096]{1,0:T(8,128)S(1)}, /*i...) while((s32[]{:T(128)}, f32[16,4096]{1,0:T(8,128)S(1)}, ...), condition=%wide.region_7.8_spmd, body=%wide.region_6.7_spmd.sunk | while | flops 1114114 | bytes 3932281 | solution.py:19
  251.6 1.5 fusion.37
  253.1 1.5 fusion.37
  254.6 1.5 fusion.37
  256.1 1.5 fusion.37
  257.6 1.5 fusion.37
  (60 shorter events, 16.4 us)
Async XLA Ops:
  7.2 121.5 %all-gather.8.cloned.1.call-start = ((), (), s32[]{:S(2)}) async-start(), calls=%async_computation.1 | async-start | bytes 2359296 | tf_op jit(solution)/shard_map/all_gather | solution.py:16
  100.0 58.3 %all-gather.10.cloned.1.call-start = ((), (), s32[]{:S(2)}) async-start(), calls=%async_computation.2 | async-start | bytes 2359296 | tf_op jit(solution)/shard_map/all_gather | solution.py:16
  100.9 87.2 %all-gather.12.cloned.1.call-start = ((), (), s32[]{:S(2)}) async-start(), calls=%async_computation.3 | async-start | bytes 2359296 | tf_op jit(solution)/shard_map/all_gather | solution.py:16
  101.7 116.4 %all-gather.6.cloned.1.call-start = ((), (), s32[]{:S(2)}) async-start(), calls=%async_computation | async-start | bytes 2359296 | tf_op jit(solution)/shard_map/all_gather | solution.py:16
  102.6 145.1 %all-gather.14.cloned.1.call-start = ((), (), s32[]{:S(2)}) async-start(), calls=%async_computation.4 | async-start | bytes 2359296 | tf_op jit(solution)/shard_map/all_gather | solution.py:16
  190.9 32.1 %copy-start = (f32[8,16,4096]{2,1,0:T(8,128)S(1)}, f32[8,16,4096]{2,1,0:T(8,128)}, u32[]{:S(2)}) copy-start(f32[8,16,4096]{2,1,0:T(8,128)} %all-gather.8.cloned.1.call-done) | copy-start | bytes 6291460
  224.0 27.6 %slice-start = ((f32[8,16,4096]{2,1,0:T(8,128)}), f32[7,16,4096]{2,1,0:T(8,128)S(1)}, s32[]{:S(2)}) async-start(f32[8,16,4096]{2,1,0:T(8,128)} %all-gather.8.cloned.1.call-done), calls=%async_computation.5 | async-start | bytes 3670016 | tf_op jit(solution)/shard_map/slice | solution.py:18
Sparse Core Ops, SparseCore 0:
  100.2 28.4 all-gather.7
  130.5 27.7 all-gather.9
  160.2 27.7 all-gather.11
  190.4 27.7 all-gather.5
  219.9 27.7 all-gather.13
where the time goes:
time: 272 us; the launch traced here: 270 us
  waiting for transfers between devices  130 us (48%)
  local copies, waits for them, and re-layouts  64.7 us (24%)
  other arithmetic  27.8 us (10%)
  matrix products  22.6 us (8%)
  between operations  14 us (5%)
  blocking collectives  10.9 us (4%)
    all_gather x5, waiting for transfers between devices, merged(): pieces = jax.tree.map(lambda part: lax.all_gather(part, axis), value)  130 us
    reshape x2, local copies, waits for them, and re-layouts, body(): score = score.reshape(local_tmpl, flat_rows, doubled)  24.9 us
    dot_general x1, matrix products, body(): jnp.dot(spectrum.reshape(local_tmpl * flat_rows, 2 * doubled), paired_tab...  22.6 us
    reshape x1, local copies, waits for them, and re-layouts, body(): spectrum.reshape(local_tmpl * flat_rows, 2 * doubled)  19.1 us
    max x12, other arithmetic, merge_top(): jnp.maximum(winner, jnp.minimum(former[rank_in], latter[rank_out - rank_i...  12.7 us
    slice x6, local copies, waits for them, and re-layouts, merged(): tail = jax.tree.map(lambda part: part[1:], pieces)  11.6 us
    psum x1, blocking collectives, body(): sum_plain, sum_square = lax.psum((sum_plain, sum_square), 'grid')  10.9 us
  transfers between devices with their start and end apart: 5, of which 5 were waited for; matrix products, arithmetic and copies ran while one was open for 6% of the time, Pallas kernels for 0%

commit v1 on v0

v1 whole, which is shorter than its diff:
```python
import functools
import math

import jax
import jax.numpy as jnp
import numpy as np
from jax import lax
from jax.experimental import pallas as pl
from jax.experimental.pallas import tpu as pltpu
from jax.sharding import PartitionSpec as P

TOP = 4
KEPT = TOP + 1
SPREAD_FLOOR = 0.25
CHUNKS = 4
BATCH = 2
MESH = pl.DeviceIdType.MESH


def phase_tables(points):
    order = np.arange(points)
    angle = (order[:, None] * order[None, :] % points) * (2.0 * math.pi / points)
    table = np.concatenate([np.cos(angle), -np.sin(angle)], axis=0)
    table = np.kron(np.eye(2), table).astype(np.float32)
    lead = table.astype(jnp.bfloat16)
    rest = (table - lead.astype(np.float32)).astype(jnp.bfloat16)
    return np.concatenate([lead, lead, rest], axis=0)


def order_pair(former, latter):
    return jnp.maximum(former, latter), jnp.minimum(former, latter)


def order_four(values):
    a, b = order_pair(values[0], values[1])
    c, d = order_pair(values[2], values[3])
    a, c = order_pair(a, c)
    b, d = order_pair(b, d)
    b, c = order_pair(b, c)
    return [a, b, c, d]


def merge_four(former, latter):
    a, b, c, d = (jnp.maximum(former[i], latter[TOP - 1 - i]) for i in range(TOP))
    a, c = order_pair(a, c)
    b, d = order_pair(b, d)
    a, b = order_pair(a, b)
    c, d = order_pair(c, d)
    return [a, b, c, d]


def merge_groups(former, latter):
    return merge_four(former[:TOP], latter[:TOP]) + [former[TOP] + latter[TOP]]


def kernel(
    groups, slabs, parts,
    spectrum_ref, table_ref, best_ref, coherence_ref,
    held, table, score, stats, gathered, average, scale, leaders, sibling, merged, arrived,
    held_sem, table_sem, stats_send, stats_recv, pair_send, pair_recv, far_send, far_recv,
):
    local_tmpl, slab_rows, beta_rows, doubled = spectrum_ref.shape
    points = doubled // 2
    half = slab_rows // 2
    chips = groups // 2
    piece = beta_rows // groups
    per_chunk = half // CHUNKS
    cell_count = float(points * points * points)

    place = lax.axis_index("tmpl")
    slab = lax.axis_index("grid")
    chip, core = place // 2, place % 2

    def fetch(number):
        return pltpu.make_async_copy(
            spectrum_ref.at[pl.ds(number * BATCH, BATCH)],
            held.at[pl.ds(number * BATCH, BATCH)],
            held_sem.at[number],
        )

    bring_table = pltpu.make_async_copy(table_ref, table, table_sem)
    bring_table.start()
    for number in range(local_tmpl // BATCH):
        fetch(number).start()

    partner = (2 * chip + 1 - core, slab)
    far = [(2 * ((chip + step) % chips) + core, slab) for step in range(1, chips)]
    near = [(place, (slab + step) % slabs) for step in range(1, slabs)]
    barrier = pltpu.get_barrier_semaphore()
    for device in [partner] + far + near:
        pl.semaphore_signal(barrier, inc=1, device_id=device, device_id_type=MESH)

    bring_table.wait()

    def transform(number, carry):
        fetch(number).wait()
        base = number * BATCH
        rows = BATCH * half * beta_rows
        leads, rests = [], []
        for side in range(2):
            coeffs = held[pl.ds(base, BATCH), pl.ds(side * half, half)].reshape(rows, doubled)
            lead = coeffs.astype(jnp.bfloat16)
            leads.append(lead)
            rests.append((coeffs - lead.astype(jnp.float32)).astype(jnp.bfloat16))
        value = jnp.dot(
            jnp.concatenate(leads + rests + leads, axis=1),
            table[...],
            preferred_element_type=jnp.float32,
        )
        value = value.reshape(BATCH, half, beta_rows, doubled)
        score[pl.ds(base, BATCH)] = value
        for index in range(BATCH):
            one = value[index].reshape(half * beta_rows // 8, 8, doubled)
            plain = jnp.sum(jnp.sum(one, axis=0), axis=0, keepdims=True)
            square = jnp.sum(jnp.sum(one * one, axis=0), axis=0, keepdims=True)
            stats[0, pl.ds(base + index, 1)] = plain
            stats[1, pl.ds(base + index, 1)] = square
        return carry

    def share_stats(part):
        low, high = parts[part], parts[part + 1]
        return [
            pltpu.make_async_remote_copy(
                src_ref=stats.at[:, pl.ds(low, high - low)],
                dst_ref=gathered.at[step, :, pl.ds(low, high - low)],
                send_sem=stats_send.at[part, step],
                recv_sem=stats_recv.at[part, step],
                device_id=near[step],
                device_id_type=MESH,
            )
            for step in range(slabs - 1)
        ]

    def settle(part):
        low, size = parts[part], parts[part + 1] - parts[part]
        total = stats[:, pl.ds(low, size)]
        for step, copy in enumerate(share_stats(part)):
            copy.wait_recv()
            total = total + gathered[step, :, pl.ds(low, size)]
        total = jnp.sum(total, axis=-1, keepdims=True) / cell_count
        mean = total[0]
        spread = total[1] - mean * mean
        factor = 1.0 / jnp.sqrt(spread + SPREAD_FLOOR)
        average[pl.ds(low, size)] = jnp.broadcast_to(mean, (size, doubled))
        scale[pl.ds(low, size)] = jnp.broadcast_to(factor, (size, doubled))

    def leading(part, chunk):
        low, high = parts[part], parts[part + 1]

        def one_row(row, carry):
            line = chunk * per_chunk + row
            for pair in range(chips):
                window = pl.ds(pair * 2 * piece, 2 * piece)
                running = None
                for base in range(low, high, TOP):
                    values = []
                    for tmpl in range(base, base + TOP):
                        centred = score[tmpl, line, window] - average[pl.ds(tmpl, 1)]
                        values.append(centred * scale[pl.ds(tmpl, 1)])
                    summed = (values[0] + values[1]) + (values[2] + values[3])
                    fresh = order_four(values) + [summed]
                    running = fresh if running is None else merge_groups(running, fresh)
                for side in range(2):
                    rows = slice(side * piece, (side + 1) * piece)
                    mine = [value[rows] for value in running]
                    if part > 0:
                        former = [leaders[chunk, side, pair, rank, row] for rank in range(KEPT)]
                        mine = merge_groups(former, mine)
                    for rank in range(KEPT):
                        leaders[chunk, side, pair, rank, row] = mine[rank]
            return carry

        lax.fori_loop(0, per_chunk, one_row, 0)

    def exchange(chunk):
        return pltpu.make_async_remote_copy(
            src_ref=leaders.at[chunk, 1 - core],
            dst_ref=sibling.at[chunk],
            send_sem=pair_send.at[chunk],
            recv_sem=pair_recv.at[chunk],
            device_id=partner,
            device_id_type=MESH,
        )

    def scatter(chunk):
        return [
            pltpu.make_async_remote_copy(
                src_ref=merged.at[chunk, (chip + step) % chips],
                dst_ref=arrived.at[chunk, step - 1],
                send_sem=far_send.at[chunk, step - 1],
                recv_sem=far_recv.at[chunk, step - 1],
                device_id=far[step - 1],
                device_id_type=MESH,
            )
            for step in range(1, chips)
        ]

    def join_pair(chunk):
        exchange(chunk).wait_recv()
        for pair in range(chips):
            former = [leaders[chunk, core, pair, rank] for rank in range(KEPT)]
            latter = [sibling[chunk, pair, rank] for rank in range(KEPT)]
            for rank, value in enumerate(merge_groups(former, latter)):
                merged[chunk, pair, rank] = value
        for copy in scatter(chunk):
            copy.start()

    def finish(chunk):
        running = [merged[chunk, chip, rank] for rank in range(KEPT)]
        for step, copy in enumerate(scatter(chunk)):
            copy.wait_recv()
            running = merge_groups(
                running, [arrived[chunk, step, rank] for rank in range(KEPT)]
            )
        running[TOP] = running[TOP] / math.sqrt(groups * local_tmpl)
        for side in range(2):
            rows = pl.ds(side * half + chunk * per_chunk, per_chunk)
            lanes = slice(side * points, (side + 1) * points)
            for rank in range(TOP):
                best_ref[rank, rows] = running[rank][..., lanes]
            coherence_ref[rows] = running[TOP][..., lanes]

    count = len(parts) - 1
    for part in range(count):
        lax.fori_loop(parts[part] // BATCH, parts[part + 1] // BATCH, transform, 0)
        if part == 0:
            pl.semaphore_wait(barrier, 1 + len(far) + len(near))
        for copy in share_stats(part):
            copy.start()
    for part in range(count - 1):
        settle(part)
        for chunk in range(CHUNKS):
            leading(part, chunk)
    settle(count - 1)
    for chunk in range(CHUNKS):
        leading(count - 1, chunk)
        exchange(chunk).start()
        if chunk > 0:
            join_pair(chunk - 1)
    join_pair(CHUNKS - 1)
    for chunk in range(CHUNKS):
        finish(chunk)
    for part in range(count):
        for copy in share_stats(part):
            copy.wait_send()
    for chunk in range(CHUNKS):
        exchange(chunk).wait_send()
        for copy in scatter(chunk):
            copy.wait_send()


def body(groups, slabs, spectrum):
    local_tmpl, slab_rows, beta_rows, doubled = spectrum.shape
    points = doubled // 2
    half = slab_rows // 2
    chips = groups // 2
    piece = beta_rows // groups
    per_chunk = half // CHUNKS
    parts = (0, local_tmpl * 3 // 4, local_tmpl)
    count = len(parts) - 1
    block = (chips, KEPT, per_chunk, piece, doubled)
    f32 = jnp.float32
    dma = pltpu.SemaphoreType.DMA
    return pl.pallas_call(
        functools.partial(kernel, groups, slabs, parts),
        out_shape=(
            jax.ShapeDtypeStruct((TOP, slab_rows, piece, points), f32),
            jax.ShapeDtypeStruct((slab_rows, piece, points), f32),
        ),
        in_specs=[pl.BlockSpec(memory_space=pltpu.HBM)] * 2,
        out_specs=(
            pl.BlockSpec(memory_space=pltpu.VMEM),
            pl.BlockSpec(memory_space=pltpu.VMEM),
        ),
        scratch_shapes=[
            pltpu.VMEM((local_tmpl, slab_rows, beta_rows, doubled), f32),
            pltpu.VMEM((6 * doubled, doubled), jnp.bfloat16),
            pltpu.VMEM((local_tmpl, half, beta_rows, doubled), f32),
            pltpu.VMEM((2, local_tmpl, doubled), f32),
            pltpu.VMEM((slabs - 1, 2, local_tmpl, doubled), f32),
            pltpu.VMEM((local_tmpl, doubled), f32),
            pltpu.VMEM((local_tmpl, doubled), f32),
            pltpu.VMEM((CHUNKS, 2) + block, f32),
            pltpu.VMEM((CHUNKS,) + block, f32),
            pltpu.VMEM((CHUNKS,) + block, f32),
            pltpu.VMEM((CHUNKS, chips - 1) + block[1:], f32),
            dma((local_tmpl // BATCH,)),
            dma,
            dma((count, slabs - 1)),
            dma((count, slabs - 1)),
            dma((CHUNKS,)),
            dma((CHUNKS,)),
            dma((CHUNKS, chips - 1)),
            dma((CHUNKS, chips - 1)),
        ],
        compiler_params=pltpu.CompilerParams(
            collective_id=0, has_side_effects=True, vmem_limit_bytes=60 * 1024 * 1024
        ),
    )(spectrum, jnp.asarray(phase_tables(points)))


def solution(mesh):
    return jax.shard_map(
        functools.partial(body, mesh.shape["tmpl"], mesh.shape["grid"]),
        mesh=mesh,
        in_specs=(P("tmpl", "grid", None, None),),
        out_specs=(P(None, "grid", "tmpl", None), P("grid", "tmpl", None)),
        check_vma=False,
    )
```

time: 272 us -> 37.4 us (0.14)
  waiting for transfers between devices: 130 us -> 0 us
  local copies, waits for them, and re-layouts: 64.7 us -> 3.14 us
  Pallas kernels: 0 us -> 33.4 us
  other arithmetic: 27.8 us -> 0 us
  matrix products: 22.6 us -> 0 us
  between operations: 14 us -> 0.64 us
  blocking collectives: 10.9 us -> 0 us
    all_gather x5 -> x0, waiting for transfers between devices: 130 us -> none  [merged(): pieces = jax.tree.map(lambda part: lax.all_gather(part, axis), value)]
    reshape x4 -> x0, local copies, waits for them, and re-layouts: 44.7 us -> none  [the longest x2 24.9 us: body(): score = score.reshape(local_tmpl, flat_rows, doubled)]
    pallas_call x0 -> x1, Pallas kernels: none -> 33.4 us  [body(): pl.pallas_call(functools.partial(kernel, groups, slabs, parts), out_shape...]
    dot_general x1 -> x0, matrix products: 22.6 us -> none  [body(): jnp.dot(spectrum.reshape(local_tmpl * flat_rows, 2 * doubled), paired_tab...]
    max x14 -> x0, other arithmetic: 12.8 us -> none  [the longest x12 12.7 us: merge_top(): jnp.maximum(winner, jnp.minimum(former[rank_in], latter[rank_out - rank_i...]
    slice x6 -> x0, local copies, waits for them, and re-layouts: 11.6 us -> none  [merged(): tail = jax.tree.map(lambda part: part[1:], pieces)]
    psum x1 -> x0, blocking collectives: 10.9 us -> none  [body(): sum_plain, sum_square = lax.psum((sum_plain, sum_square), 'grid')]
    add x5 -> x0, other arithmetic: 5.26 us -> none  [fold_levels(): running = folded[:, 0] + folded[:, 1]]
  transfers between devices with their start and end apart: 5 -> 0, of which waited for: 5 -> 0; matrix products, arithmetic and copies ran while one was open for 6% -> 0% of each run, Pallas kernels for 0% -> 0%
where the time goes in v1:
time: 37.4 us; the launch traced here: 37.2 us
  Pallas kernels  33.4 us (89%)
  local copies, waits for them, and re-layouts  3.14 us (8%)
  between operations  0.64 us (2%)
    pallas_call x1, Pallas kernels, body(): pl.pallas_call(functools.partial(kernel, groups, slabs, parts), out_shape...  33.4 us
    unnamed x2, local copies, waits for them, and re-layouts  3.14 us

profile of v1, /device:TPU:1, one launch (start us, length us, event | category | flops | bytes accessed | tf_op | source)
XLA Modules:
  0.0 37.2 jit_solution(12560689934670698179)
XLA Ops:
  0.6 33.4 %shard_map.41 = (f32[4,16,8,64]{3,2,1,0:T(8,128)}, f32[16,8,64]{2,1,0:T(8,128)}) custom-call(f32[32,16,64,128]{3,2,1,0:T(8,128)} %spectrum_ref.1, bf16[768,128]{1,0:T(8,128)(2,1)} %constant.2.clone.table_ref), custom_call_target="tpu_custom_call" | custom-call | tf_op jit(solution)/shard_map/pallas_call | solution.py:264
  34.0 1.7 %copy.6 = f32[4,16,8,64]{3,2,1,0:T(8,128)} copy(f32[4,16,8,64]{3,2,1,0:T(8,128)} %get-tuple-element.4) | data formatting | bytes 262144
  35.7 1.5 %copy.7 = f32[16,8,64]{2,1,0:T(8,128)} copy(f32[16,8,64]{2,1,0:T(8,128)} %get-tuple-element.5) | data formatting | bytes 65536

commit v2 on v1

--- a/solution.py
+++ b/solution.py
@@ -13,7 +13,9 @@
 KEPT = TOP + 1
 SPREAD_FLOOR = 0.25
 CHUNKS = 4
-BATCH = 2
+BATCH = 8
+AHEAD = 4
+MB = 256
 MESH = pl.DeviceIdType.MESH
 
 
@@ -24,7 +26,7 @@
     table = np.kron(np.eye(2), table).astype(np.float32)
     lead = table.astype(jnp.bfloat16)
     rest = (table - lead.astype(np.float32)).astype(jnp.bfloat16)
-    return np.concatenate([lead, lead, rest], axis=0)
+    return np.concatenate([lead, rest], axis=1)
 
 
 def order_pair(former, latter):
@@ -55,7 +57,7 @@
 
 def kernel(
     groups, slabs, parts,
-    spectrum_ref, table_ref, best_ref, coherence_ref,
+    spectrum_ref, table_ref, packed_ref,
     held, table, score, stats, gathered, average, scale, leaders, sibling, merged, arrived,
     held_sem, table_sem, stats_send, stats_recv, pair_send, pair_recv, far_send, far_recv,
 ):
@@ -80,7 +82,7 @@
 
     bring_table = pltpu.make_async_copy(table_ref, table, table_sem)
     bring_table.start()
-    for number in range(local_tmpl // BATCH):
+    for number in range(min(AHEAD, local_tmpl // BATCH)):
         fetch(number).start()
 
     partner = (2 * chip + 1 - core, slab)
@@ -94,27 +96,32 @@
 
     def transform(number, carry):
         fetch(number).wait()
+
+        @pl.when(number + AHEAD < local_tmpl // BATCH)
+        def _():
+            fetch(number + AHEAD).start()
+
         base = number * BATCH
-        rows = BATCH * half * beta_rows
-        leads, rests = [], []
-        for side in range(2):
-            coeffs = held[pl.ds(base, BATCH), pl.ds(side * half, half)].reshape(rows, doubled)
-            lead = coeffs.astype(jnp.bfloat16)
-            leads.append(lead)
-            rests.append((coeffs - lead.astype(jnp.float32)).astype(jnp.bfloat16))
-        value = jnp.dot(
-            jnp.concatenate(leads + rests + leads, axis=1),
-            table[...],
-            preferred_element_type=jnp.float32,
-        )
-        value = value.reshape(BATCH, half, beta_rows, doubled)
-        score[pl.ds(base, BATCH)] = value
+        lines = MB // beta_rows
         for index in range(BATCH):
-            one = value[index].reshape(half * beta_rows // 8, 8, doubled)
-            plain = jnp.sum(jnp.sum(one, axis=0), axis=0, keepdims=True)
-            square = jnp.sum(jnp.sum(one * one, axis=0), axis=0, keepdims=True)
-            stats[0, pl.ds(base + index, 1)] = plain
-            stats[1, pl.ds(base + index, 1)] = square
+            plain = square = None
+            for block in range(half // lines):
+                leads, rests = [], []
+                for side in range(2):
+                    coeffs = held[base + index, pl.ds(side * half + block * lines, lines)].reshape(MB, doubled)
+                    lead = coeffs.astype(jnp.bfloat16)
+                    leads.append(lead)
+                    rests.append((coeffs - lead.astype(jnp.float32)).astype(jnp.bfloat16))
+                both = jnp.dot(jnp.concatenate(leads, axis=1), table[...], preferred_element_type=jnp.float32)
+                value = both[:, :doubled] + both[:, doubled:] + jnp.dot(jnp.concatenate(rests, axis=1), table[:, :doubled], preferred_element_type=jnp.float32)
+                score[base + index, pl.ds(block * lines, lines)] = value.reshape(lines, beta_rows, doubled)
+                one = value.reshape(MB // 8, 8, doubled)
+                p = jnp.sum(one, axis=0)
+                q = jnp.sum(one * one, axis=0)
+                plain = p if plain is None else plain + p
+                square = q if square is None else square + q
+            stats[0, pl.ds(base + index, 1)] = jnp.sum(plain, axis=0, keepdims=True)
+            stats[1, pl.ds(base + index, 1)] = jnp.sum(square, axis=0, keepdims=True)
         return carry
 
     def share_stats(part):
@@ -213,12 +220,8 @@
                 running, [arrived[chunk, step, rank] for rank in range(KEPT)]
             )
         running[TOP] = running[TOP] / math.sqrt(groups * local_tmpl)
-        for side in range(2):
-            rows = pl.ds(side * half + chunk * per_chunk, per_chunk)
-            lanes = slice(side * points, (side + 1) * points)
-            for rank in range(TOP):
-                best_ref[rank, rows] = running[rank][..., lanes]
-            coherence_ref[rows] = running[TOP][..., lanes]
+        for rank in range(KEPT):
+            packed_ref[rank, pl.ds(chunk * per_chunk, per_chunk)] = running[rank]
 
     count = len(parts) - 1
     for part in range(count):
@@ -249,6 +252,15 @@
             copy.wait_send()
 
 
+def unpack(packed_ref, best_ref, coherence_ref):
+    half, points = packed_ref.shape[1], best_ref.shape[-1]
+    for side in range(2):
+        rows = pl.ds(side * half, half)
+        lanes = slice(side * points, (side + 1) * points)
+        best_ref[:, rows] = packed_ref[:TOP, :, :, lanes]
+        coherence_ref[rows] = packed_ref[TOP, :, :, lanes]
+
+
 def body(groups, slabs, spectrum):
     local_tmpl, slab_rows, beta_rows, doubled = spectrum.shape
     points = doubled // 2
@@ -256,25 +268,19 @@
     chips = groups // 2
     piece = beta_rows // groups
     per_chunk = half // CHUNKS
-    parts = (0, local_tmpl * 3 // 4, local_tmpl)
+    parts = (0, local_tmpl // 2, local_tmpl)
     count = len(parts) - 1
     block = (chips, KEPT, per_chunk, piece, doubled)
     f32 = jnp.float32
     dma = pltpu.SemaphoreType.DMA
-    return pl.pallas_call(
+    packed = pl.pallas_call(
         functools.partial(kernel, groups, slabs, parts),
-        out_shape=(
-            jax.ShapeDtypeStruct((TOP, slab_rows, piece, points), f32),
-            jax.ShapeDtypeStruct((slab_rows, piece, points), f32),
-        ),
+        out_shape=jax.ShapeDtypeStruct((KEPT, half, piece, doubled), f32),
         in_specs=[pl.BlockSpec(memory_space=pltpu.HBM)] * 2,
-        out_specs=(
-            pl.BlockSpec(memory_space=pltpu.VMEM),
-            pl.BlockSpec(memory_space=pltpu.VMEM),
-        ),
+        out_specs=pl.BlockSpec(memory_space=pltpu.VMEM),
         scratch_shapes=[
             pltpu.VMEM((local_tmpl, slab_rows, beta_rows, doubled), f32),
-            pltpu.VMEM((6 * doubled, doubled), jnp.bfloat16),
+            pltpu.VMEM((2 * doubled, 2 * doubled), jnp.bfloat16),
             pltpu.VMEM((local_tmpl, half, beta_rows, doubled), f32),
             pltpu.VMEM((2, local_tmpl, doubled), f32),
             pltpu.VMEM((slabs - 1, 2, local_tmpl, doubled), f32),
@@ -297,6 +303,13 @@
             collective_id=0, has_side_effects=True, vmem_limit_bytes=60 * 1024 * 1024
         ),
     )(spectrum, jnp.asarray(phase_tables(points)))
+    return pl.pallas_call(
+        unpack,
+        out_shape=(
+            jax.ShapeDtypeStruct((TOP, slab_rows, piece, points), f32),
+            jax.ShapeDtypeStruct((slab_rows, piece, points), f32),
+        ),
+    )(packed)
 
 
 def solution(mesh):

time: 37.4 us -> 30.7 us (0.82)
  Pallas kernels: 33.4 us -> 29.9 us
  local copies, waits for them, and re-layouts: 3.14 us -> 0 us
    pallas_call x1, Pallas kernels: 33.4 us -> 28.2 us  [body(): pl.pallas_call(functools.partial(kernel, groups, slabs, parts), out_shape...]
    unnamed x2 -> x0, local copies, waits for them, and re-layouts: 3.14 us -> none
    pallas_call x0 -> x1, Pallas kernels: none -> 1.73 us  [body(): pl.pallas_call(unpack, out_shape=(jax.ShapeDtypeStruct((TOP, slab_rows, p...]
where the time goes in v2:
time: 30.7 us; the launch traced here: 30.5 us
  Pallas kernels  29.9 us (97%)
  between operations  0.64 us (2%)
    pallas_call x1, Pallas kernels, body(): pl.pallas_call(functools.partial(kernel, groups, slabs, parts), out_shape...  28.2 us
    pallas_call x1, Pallas kernels, body(): pl.pallas_call(unpack, out_shape=(jax.ShapeDtypeStruct((TOP, slab_rows, p...  1.73 us

profile of v2, /device:TPU:1, one launch (start us, length us, event | category | flops | bytes accessed | tf_op | source)
XLA Modules:
  0.0 30.5 jit_solution(6184560523720159159)
XLA Ops:
  0.6 28.2 %shard_map.41.packed_ref = f32[5,8,8,128]{3,2,1,0:T(8,128)} custom-call(f32[32,16,64,128]{3,2,1,0:T(8,128)} %spectrum_ref.1, bf16[256,256]{1,0:T(8,128)(2,1)} %constant.2.clone.table_ref), custom_call_target="tpu_custom_call" | custom-call | tf_op jit(solution)/shard_map/pallas_call | solution.py:276
  28.8 1.7 %shard_map.42 = (f32[4,16,8,64]{3,2,1,0:T(8,128)}, f32[16,8,64]{2,1,0:T(8,128)}) custom-call(f32[5,8,8,128]{3,2,1,0:T(8,128)} %shard_map.41.packed_ref), custom_call_target="tpu_custom_call" | custom-call | tf_op jit(solution)/shard_map/pallas_call | solution.py:306
